TPU v7x, 32 devices: a whole 2x2x4 slice. The times are simulated.
32 devices in a mesh: gx: 16 (over z, y, core), gy: 2 (over x).
Axes of the slice: x: 2, y: 2, z: 4, core: 2. Of those that a mesh axis runs over, the one named last changes fastest.
Arguments:
- right_side: float32 [16, 2, 512, 256], P('gx', 'gy'), may hold values from -8 to 8, as said below
- coords: float32 [16, 2, 2, 512], P('gx', 'gy'), may hold values from 0 to 1
- noise: float32 [16, 2, 512], P('gx', 'gy'), may hold values from 0.25 to 1
- intersect: int32 [16, 2, 128], P('gx', 'gy'), may hold values from 0 to 4607, as said below
Outputs:
- solution: float32 [16, 2, 512, 256], P('gx', 'gy')
- residual: float32 [16, 2, 512, 256], P('gx', 'gy')
Inputs may be any that keep to these rules, and one draw needn't show every extreme that they name: `right_side`: right-hand sides of order one. `intersect`: each subdomain's list holds 128 distinct indices in increasing order; none names the subdomain itself (block number 4) or a subdomain beyond the first or last one along the second dimension.
All inputs are finite; a program needn't handle non-finite values.
Results may differ from a plain program's by a relative error of at most 0.0003.
Values sent between devices are 32-bit elements; how exact they have to be, the bound alone decides.
A program may use at most 128 MiB of HBM per device.

v0:
```python
import functools
import math

import jax
import jax.numpy as jnp
from jax import lax
from jax.experimental import pallas as pl
from jax.experimental.pallas import tpu as pltpu
from jax.sharding import PartitionSpec as P

ITERS = 3


RANGE_LEN = 0.25
ROOT_THREE = math.sqrt(3.0)
HIGH = lax.Precision.HIGHEST


def shifted(value, axis, by):
    count = lax.axis_size(axis)
    return lax.ppermute(value, axis, [(i, (i + by) % count) for i in range(count)])


def passed_along(block, axis, distance):
    devices = range(lax.axis_size(axis))
    route = [(i - distance, i) for i in devices if i - distance in devices]
    return lax.ppermute(block, axis, route)


def kernel_block(rows_pos, cols_pos):
    delta_x = rows_pos[0][:, None] - cols_pos[0][None, :]
    delta_y = rows_pos[1][:, None] - cols_pos[1][None, :]
    distance = jnp.sqrt(delta_x * delta_x + delta_y * delta_y)
    scaled = ROOT_THREE / RANGE_LEN * distance
    clipped = jnp.minimum(distance, 1.0)
    taper_val = jnp.square(jnp.square(1.0 - clipped)) * (4.0 * clipped + 1.0)
    return (1.0 + scaled) * jnp.exp(-scaled) * taper_val


def window_values(values):
    beside = {}
    for step_by in (1, -1):
        beside[step_by] = shifted(values, "gx", step_by)
    column = jnp.stack([beside[1], values, beside[-1]])
    across = {}
    for step_by in (1, -1):
        across[step_by] = passed_along(column, "gy", step_by)
    return [across[1], column, across[-1]]


CHUNKS = 4
MESH = pl.DeviceIdType.MESH
NOISE_MIN = 0.25
VMEM = pl.BlockSpec(memory_space=pltpu.VMEM)


def split(value):
    top = value.astype(jnp.bfloat16)
    return top, (value - top.astype(jnp.float32)).astype(jnp.bfloat16)


def dot3(left, right):
    left_top, left_low = split(left)
    right_top, right_low = split(right)
    return jnp.dot(
        jnp.concatenate([left_top, left_top, left_low], axis=1),
        jnp.concatenate([right_top, right_low, right_top], axis=0),
        preferred_element_type=jnp.float32,
    )


def dot6(left, right):
    return jnp.dot(left, right, precision=HIGH, preferred_element_type=jnp.float32)


def block_inverse(block):
    size = block.shape[0]
    low, high = NOISE_MIN * 0.97, (size + 1.0) * 1.01
    eye = (
        lax.broadcasted_iota(jnp.int32, block.shape, 0)
        == lax.broadcasted_iota(jnp.int32, block.shape, 1)
    ).astype(jnp.float32)
    first = 2.0 / (low + high)
    gap = 1.0 - first * low
    scale = 2.0 / (2.0 - gap * gap)
    guess = (2.0 * first * scale) * eye - (first * first * scale) * block
    gap = gap * gap / (2.0 - gap * gap)
    while gap > 1e-3:
        scale = 2.0 / (2.0 - gap * gap)
        rest = 2.0 * eye - dot3(block, guess)
        guess = scale * dot3(guess, rest)
        gap = gap * gap / (2.0 - gap * gap)
    for _ in range(2):
        guess = guess + dot3(guess, eye - dot6(block, guess))
    return guess


def invert(matrix_ref, out_ref):
    size = matrix_ref.shape[0]
    step = math.gcd(size, 128)
    out_ref[...] = matrix_ref[...]
    for start in range(0, size, step):
        here = slice(start, start + step)
        pivot = block_inverse(out_ref[here, here])
        column = out_ref[:, here]
        row = dot6(pivot, out_ref[here, :])
        for low in range(0, size, step):
            if low != start:
                part = slice(low, low + step)
                out_ref[part, :] = out_ref[part, :] - dot6(column[part], row)
                out_ref[part, here] = -dot6(column[part], pivot)
        out_ref[here, :] = row
        out_ref[here, here] = pivot


def columns_of(count):
    return () if count == 1 else (1,) if count == 2 else (-1, 1)


def opposite(col_off, count):
    return col_off if count == 2 else -col_off


def offsets_of(count):
    near = [(-1, 0), (1, 0)]
    for col_off in columns_of(count):
        near += [(0, col_off), (-1, col_off), (1, col_off)]
    return near


def cg_kernel(
    rhs_ref, window_ref, matrix_ref, pick_ref, put_ref,
    solution_ref, residual_ref,
    top_ref, low_ref, inverse, inv_top_ref, inv_low_ref, asked, got, tail, back, precond, window, direction, image, mine, slots_y, slots_x,
    send_sem, recv_sem,
):
    size_x, size_y = lax.axis_size("gx"), lax.axis_size("gy")
    my_x, my_y = lax.axis_index("gx"), lax.axis_index("gy")
    near = offsets_of(size_y)
    points = rhs_ref.shape[0]
    borrowed = tail.shape[0]
    half = points // CHUNKS

    def inside(col_off):
        if col_off == 0 or size_y == 2:
            return None
        return my_y > 0 if col_off < 0 else my_y < size_y - 1

    def guarded(condition, action):
        if condition is None:
            action()
        else:
            pl.when(condition)(action)

    def target(row_off, col_off):
        place = {}
        if row_off:
            place["gx"] = lax.rem(my_x + row_off + size_x, size_x)
        if col_off:
            place["gy"] = 1 - my_y if size_y == 2 else my_y + col_off
        return place

    counter = [0]

    class Move:
        def __init__(self, source, dest, row_off, col_off):
            index = counter[0]
            counter[0] += 1
            self.copy = pltpu.make_async_remote_copy(
                src_ref=source,
                dst_ref=dest,
                send_sem=send_sem.at[index],
                recv_sem=recv_sem.at[index],
                device_id=target(row_off, col_off),
                device_id_type=MESH,
            )
            self.out = inside(col_off)
            self.into = inside(-col_off)

        def start(self):
            guarded(self.out, self.copy.start)

        def sent(self):
            guarded(self.out, self.copy.wait_send)

        def landed(self):
            guarded(self.into, self.copy.wait_recv)

    def slot(row_off, col_off):
        return near.index((-row_off, opposite(col_off, size_y)))

    barrier = pltpu.get_barrier_semaphore()
    greeted = 0
    for axis, here, count in (("gx", my_x, size_x), ("gy", my_y, size_y)):
        for hop in range(1, count):
            pl.semaphore_signal(
                barrier, inc=1, device_id={axis: lax.rem(here + hop, count)}, device_id_type=MESH
            )
            greeted += 1
    for row_off, col_off in near:
        if row_off and col_off:

            def greet(row_off=row_off, col_off=col_off):
                pl.semaphore_signal(
                    barrier, inc=1, device_id=target(row_off, col_off), device_id_type=MESH
                )

            guarded(inside(col_off), greet)
            there = inside(col_off)
            greeted = greeted + (1 if there is None else jnp.where(there, 1, 0))

    for col_off in columns_of(size_y):
        there = inside(col_off)
        if there is not None:

            def clear(col_off=col_off):
                for index, (_, col) in enumerate(near):
                    if col == col_off:
                        for iteration in range(ITERS):
                            got[iteration, index] = jnp.zeros(tail.shape, jnp.float32)
                            back[iteration, index] = jnp.zeros(tail.shape, jnp.float32)
                            window[iteration, index] = jnp.zeros(rhs_ref.shape, jnp.float32)

            pl.when(jnp.logical_not(there))(clear)

    def exact_dot(ones, value):
        top, low = split(value)
        return jnp.dot(ones, top, preferred_element_type=jnp.float32) + jnp.dot(
            ones, low, preferred_element_type=jnp.float32
        )

    def dot_parts(left_top, left_low, right):
        right_top, right_low = split(right)
        return (
            jnp.dot(left_top, right_top, preferred_element_type=jnp.float32)
            + jnp.dot(left_top, right_low, preferred_element_type=jnp.float32)
            + jnp.dot(left_low, right_top, preferred_element_type=jnp.float32)
        )

    def window_part(block, value):
        cols = slice(block * points, (block + 1) * points)
        return dot_parts(top_ref[:, cols], low_ref[:, cols], value)

    def total(iteration):
        for stage, (axis, here, count, slots) in enumerate(
            (("gy", my_y, size_y, slots_y), ("gx", my_x, size_x, slots_x))
        ):
            index = counter[0]
            counter[0] += 1
            for hop in range(1, count):
                pltpu.make_async_remote_copy(
                    src_ref=mine.at[iteration, stage],
                    dst_ref=slots.at[iteration, hop - 1],
                    send_sem=send_sem.at[index],
                    recv_sem=recv_sem.at[index],
                    device_id={axis: lax.rem(here + hop, count)},
                    device_id_type=MESH,
                ).start()
            so_far = mine[iteration, stage]
            if count > 1:
                held = slots.at[iteration]
                pltpu.make_async_copy(held, held, recv_sem.at[index]).wait()
                so_far = so_far + jnp.sum(slots[iteration], axis=0)
                pltpu.make_async_copy(held, held, send_sem.at[index]).wait()
            mine[iteration, stage + 1] = so_far
        return mine[iteration, 2]

    residual_ref[...] = rhs_ref[...]
    wait_entry = [True]
    inner_old = denominator = None
    for iteration in range(ITERS):
        requests = exact_dot(pick_ref[...], residual_ref[...])
        for index in range(len(near)):
            asked[index] = requests[index * borrowed : (index + 1) * borrowed]
        if wait_entry[0]:
            pl.semaphore_wait(barrier, greeted)
            wait_entry[0] = False
        moves = [
            Move(asked.at[index], got.at[iteration, slot(*offset)], *offset)
            for index, offset in enumerate(near)
        ]
        for move in moves:
            move.start()
        if iteration == 0:
            invert(matrix_ref, inverse)
            inv_top_ref[...], inv_low_ref[...] = split(inverse[...])
            top_ref[...], low_ref[...] = split(window_ref[...])
        solved = dot_parts(
            inv_top_ref[:, :points], inv_low_ref[:, :points], residual_ref[...]
        )
        for move in moves:
            move.landed()
        gathered = jnp.sum(got[iteration], axis=0)
        solved = solved + dot_parts(inv_top_ref[:, points:], inv_low_ref[:, points:], gathered)
        tail[...] = solved[points:]
        precond[...] = solved[:points]
        returns = [Move(tail, back.at[iteration, slot(*offset)], *offset) for offset in near]
        for move in returns:
            move.start()
        for move in moves:
            move.sent()
        for move in returns:
            move.landed()
        returned = back[iteration].reshape(len(near) * borrowed, tail.shape[1])
        precond[...] = precond[...] + exact_dot(put_ref[...], returned)
        for move in returns:
            move.sent()

        sides, relays = [], []
        for chunk in range(CHUNKS):
            rows = pl.ds(chunk * half, half)
            for col_off in columns_of(size_y):
                index = slot(0, col_off)
                sides.append(
                    Move(precond.at[rows], window.at[iteration, index, rows], 0, col_off)
                )
                sides[-1].start()
        beside = [
            Move(precond, window.at[iteration, slot(row_off, 0)], row_off, 0)
            for row_off in (-1, 1)
        ]
        for move in beside:
            move.start()
        result = window_part(len(near), precond[...])
        place = 0
        for chunk in range(CHUNKS):
            rows = pl.ds(chunk * half, half)
            for col_off in columns_of(size_y):
                sides[place].landed()
                place += 1
                source = near.index((0, opposite(col_off, size_y)))
                for row_off in (-1, 1):
                    index = near.index((-row_off, opposite(col_off, size_y)))
                    move = Move(
                        window.at[iteration, source, rows],
                        window.at[iteration, index, rows],
                        row_off,
                        0,
                    )
                    there = inside(-col_off)
                    move.out = move.into = there
                    relays.append(move)
                    move.start()
        for index, (row_off, col_off) in enumerate(near):
            if row_off == 0:
                result = result + window_part(index, window[iteration, index])
        for move in beside:
            move.landed()
        for index, (row_off, col_off) in enumerate(near):
            if row_off and col_off == 0:
                result = result + window_part(index, window[iteration, index])
        for move in relays:
            move.landed()
        for index, (row_off, col_off) in enumerate(near):
            if row_off and col_off:
                result = result + window_part(index, window[iteration, index])
        fresh = precond[...]
        mine[iteration, 0, 0:1] = jnp.sum(residual_ref[...] * fresh, axis=0, keepdims=True)
        mine[iteration, 0, 1:2] = jnp.sum(fresh * result, axis=0, keepdims=True)
        if iteration:
            mine[iteration, 0, 2:3] = jnp.sum(fresh * image[...], axis=0, keepdims=True)
        else:
            mine[iteration, 0, 2:3] = jnp.zeros((1, fresh.shape[1]), jnp.float32)
        sums = total(iteration)
        for move in sides + beside + relays:
            move.sent()
        inner, curved, mixed = sums[0:1], sums[1:2], sums[2:3]
        if iteration:
            ratio = inner / inner_old
            denominator = curved + ratio * (2.0 * mixed + ratio * denominator)
            direction[...] = fresh + ratio * direction[...]
            image[...] = result + ratio * image[...]
        else:
            denominator = curved
            direction[...] = fresh
            image[...] = result
        inner_old = inner
        step_size = inner / denominator
        moved = step_size * direction[...]
        solution_ref[...] = solution_ref[...] + moved if iteration else moved
        residual_ref[...] = residual_ref[...] - step_size * image[...]


def conjugate_gradients(right_side, window_matrix, matrix, pick):
    near = offsets_of(lax.axis_size("gy"))
    points, width = right_side.shape
    borrowed = matrix.shape[0] - points
    size_x, size_y = lax.axis_size("gx"), lax.axis_size("gy")
    sides = len(columns_of(size_y))
    moves = ITERS * (2 * len(near) + 2 + 3 * CHUNKS * sides + 2)
    out = jax.ShapeDtypeStruct(right_side.shape, jnp.float32)
    block = pltpu.VMEM((points, width), jnp.float32)
    small = (len(near), borrowed, width)
    return pl.pallas_call(
        cg_kernel,
        out_shape=(out, out),
        in_specs=[VMEM] * 5,
        out_specs=(VMEM, VMEM),
        scratch_shapes=[
            pltpu.VMEM(window_matrix.shape, jnp.bfloat16),
            pltpu.VMEM(window_matrix.shape, jnp.bfloat16),
            pltpu.VMEM(matrix.shape, jnp.float32),
            pltpu.VMEM(matrix.shape, jnp.bfloat16),
            pltpu.VMEM(matrix.shape, jnp.bfloat16),
            pltpu.VMEM(small, jnp.float32),
            pltpu.VMEM((ITERS,) + small, jnp.float32),
            pltpu.VMEM((borrowed, width), jnp.float32),
            pltpu.VMEM((ITERS,) + small, jnp.float32),
            block,
            pltpu.VMEM((ITERS, len(near), points, width), jnp.float32),
            block,
            block,
            pltpu.VMEM((ITERS, 3, 3, width), jnp.float32),
            pltpu.VMEM((ITERS, max(size_y - 1, 1), 3, width), jnp.float32),
            pltpu.VMEM((ITERS, max(size_x - 1, 1), 3, width), jnp.float32),
            pltpu.SemaphoreType.DMA((moves,)),
            pltpu.SemaphoreType.DMA((moves,)),
        ],
        compiler_params=pltpu.CompilerParams(
            collective_id=0, has_side_effects=True, vmem_limit_bytes=56 * 1024 * 1024
        ),
    )(right_side, window_matrix, matrix, pick, pick.T)


def shards(right_side, coords, noise, intersect):
    points = right_side.shape[2]
    rhs_count = right_side.shape[3]
    intersect_len = intersect.shape[2]
    ext_len = points + intersect_len
    own_pos = coords.reshape(2, points)
    own_noise = noise.reshape(points)
    listed = jnp.pad(intersect.reshape(intersect_len), (0, points - intersect_len))
    point_info = jnp.concatenate(
        [own_pos, own_noise[None, :], listed.astype(jnp.float32)[None, :]], axis=0
    )
    info_cols = window_values(point_info)
    intersect_ids = intersect.reshape(intersect_len)
    block_id = intersect_ids // points
    row_in = intersect_ids % points
    row_of = block_id // 3
    col_of = block_id % 3
    local_id = row_of * points + row_in
    picked_info = [
        jnp.take(
            jnp.transpose(info_cols[col_off], (1, 0, 2)).reshape(4, 3 * points), local_id, axis=1
        )
        for col_off in range(3)
    ]
    chosen = jnp.where(
        col_of[None, :] == 0,
        picked_info[0],
        jnp.where(col_of[None, :] == 1, picked_info[1], picked_info[2]),
    )
    ov_pos = jnp.stack(
        [chosen[0] + (row_of - 1).astype(jnp.float32), chosen[1] + (col_of - 1).astype(jnp.float32)]
    )
    ext_pos = jnp.concatenate([own_pos, ov_pos], axis=1)
    ext_noise = jnp.concatenate([own_noise, chosen[2]])
    local_matrix = kernel_block(ext_pos, ext_pos) + jnp.diag(ext_noise)
    count = lax.axis_size("gy")
    point_iota = jnp.arange(points, dtype=jnp.int32)[None, :]
    blocks, picks = [], []
    for row_off, col_off in offsets_of(count) + [(0, 0)]:
        step = col_off
        info = info_cols[col_off + 1][row_off + 1]
        if col_off and count == 2:
            first = lax.axis_index("gy") == 0
            step = jnp.where(first, 1, -1)
            info = jnp.where(first, info, info_cols[0][row_off + 1])
        shift = jnp.asarray(step, jnp.float32)
        blocks.append(
            kernel_block(own_pos, jnp.stack([info[0] + float(row_off), info[1] + shift]))
        )
        if row_off or col_off:
            ids = info[3, :intersect_len].astype(jnp.int32)
            own_rows = ids - (3 * (1 - row_off) + (1 - step)) * points
            picks.append((own_rows[:, None] == point_iota).astype(jnp.bfloat16))
    blocks[-1] = blocks[-1] + jnp.diag(own_noise)
    answer, residual = conjugate_gradients(
        right_side.reshape(points, rhs_count),
        jnp.concatenate(blocks, axis=1),
        local_matrix,
        jnp.concatenate(picks, axis=0),
    )
    return (answer.reshape(1, 1, points, rhs_count), residual.reshape(1, 1, points, rhs_count))


def split3(value):
    top = value.astype(jnp.bfloat16)
    rest = value - top.astype(jnp.float32)
    mid = rest.astype(jnp.bfloat16)
    return top, mid, (rest - mid.astype(jnp.float32)).astype(jnp.bfloat16)


def full_dot(left, right):
    lt, lm, ll = split3(left)
    rt, rm, rl = split3(right)
    return jnp.dot(
        jnp.concatenate([lt, lt, lm, lm, lt, ll], axis=1),
        jnp.concatenate([rt, rm, rt, rm, rl, rt], axis=0),
        preferred_element_type=jnp.float32,
    )


def wide(value):
    return jnp.concatenate(split(value), axis=1)


def folded(value):
    lanes = value.shape[1] // 2
    return value[:, :lanes] + value[:, lanes:]


def mm(left, right):
    return jnp.dot(left, right, preferred_element_type=jnp.float32)


def covariance(rows_x, rows_y, cols_x, cols_y):
    delta_x = rows_x - cols_x
    delta_y = rows_y - cols_y
    square = delta_x * delta_x + delta_y * delta_y
    distance = square * lax.rsqrt(jnp.maximum(square, 1e-30))
    scaled = ROOT_THREE / RANGE_LEN * distance
    rest = 1.0 - jnp.minimum(distance, 1.0)
    rest = rest * rest
    taper = rest * rest * (4.0 * jnp.minimum(distance, 1.0) + 1.0)
    return (1.0 + scaled) * jnp.exp(-scaled) * taper


def pivot_inverses(blocks):
    size = blocks[0].shape[0]
    low, high = NOISE_MIN * 0.97, (size + 1.0) * 1.01
    eye = (
        lax.broadcasted_iota(jnp.int32, blocks[0].shape, 0)
        == lax.broadcasted_iota(jnp.int32, blocks[0].shape, 1)
    ).astype(jnp.float32)
    first = 2.0 / (low + high)
    gap = 1.0 - first * low
    rests = [eye - first * block for block in blocks]
    scale = 2.0 / (2.0 - gap * gap)
    guesses = [(scale * first) * (eye + rest) for rest in rests]
    rests = [scale * full_dot(rest, rest) + (1.0 - scale) * eye for rest in rests]
    gap = gap * gap / (2.0 - gap * gap)
    while True:
        scale = 2.0 / (2.0 - gap * gap)
        gap = gap * gap / (2.0 - gap * gap)
        if gap < 1e-3:
            guesses = [
                scale * (guess + full_dot(rest, guess)) for rest, guess in zip(rests, guesses)
            ]
            break
        both = [
            full_dot(rest, jnp.concatenate([rest, guess], axis=1))
            for rest, guess in zip(rests, guesses)
        ]
        guesses = [scale * (guess + pair[:, size:]) for guess, pair in zip(guesses, both)]
        rests = [scale * pair[:, :size] + (1.0 - scale) * eye for pair in both]
    for _ in range(2):
        errors = [eye - full_dot(block, guess) for block, guess in zip(blocks, guesses)]
        guesses = [guess + dot3(guess, error) for guess, error in zip(guesses, errors)]
    return guesses


SIDES = (-1, 1)
CUTS = 4


def paired_kernel(
    rhs_ref, coords_ref, noise_ref, ids_ref,
    solution_ref, residual_ref,
    info, points_col, ext_row, ext_col, top, low, mats, inv_top, inv_low, pick, put,
    start_res, basis, images, work, work_image, accum, accum_small,
    asked, own_asked, got, tails, back, window, far, mine, slots, coef, far_coef,
    send_sem, recv_sem,
):
    size_x, size_y = lax.axis_size("gx"), lax.axis_size("gy")
    my_x, my_y = lax.axis_index("gx"), lax.axis_index("gy")
    other = 1 - my_y
    points = rhs_ref.shape[0]
    lanes = rhs_ref.shape[1] // 2
    total = 2 * points
    borrowed = ids_ref.shape[1]
    ext = points + borrowed
    row_of_side = {0: 0, -1: 1, 1: 2}

    counter = [0]
    pending = []

    def near(row_off, flip):
        place = {}
        if row_off:
            place["gx"] = lax.rem(my_x + row_off + size_x, size_x)
        if flip:
            place["gy"] = other
        return place

    def send(source, dest, row_off, flip=False):
        index = counter[0]
        counter[0] += 1
        copy = pltpu.make_async_remote_copy(
            src_ref=source,
            dst_ref=dest,
            send_sem=send_sem.at[index],
            recv_sem=recv_sem.at[index],
            device_id=near(row_off, flip),
            device_id_type=MESH,
        )
        copy.start()
        pending.append(copy)
        return copy

    half = lambda which: pl.ds(pl.multiple_of(which * lanes, lanes), lanes)
    column = lambda which: pl.ds(pl.multiple_of(which * points, points), points)

    barrier = pltpu.get_barrier_semaphore()
    for hop in range(1, size_x):
        pl.semaphore_signal(
            barrier, inc=1, device_id={"gx": lax.rem(my_x + hop, size_x)}, device_id_type=MESH
        )
    for row_off in (0, -1, 1):
        pl.semaphore_signal(barrier, inc=1, device_id=near(row_off, True), device_id_type=MESH)

    info[0, my_y] = jnp.concatenate(
        [
            coords_ref[...],
            noise_ref[...],
            jnp.concatenate(
                [
                    ids_ref[...].astype(jnp.float32),
                    jnp.zeros((1, points - borrowed), jnp.float32),
                ],
                axis=1,
            ),
            jnp.zeros((4, points), jnp.float32),
        ],
        axis=0,
    )
    start_res[column(my_y), :] = rhs_ref[:, half(my_y)]
    pl.semaphore_wait(barrier, size_x - 1 + 3)

    facts = []
    for row_off, flip in ((0, True), (-1, False), (1, False), (-1, True), (1, True)):
        dest = info.at[row_of_side[-row_off], my_y]
        facts.append(send(info.at[0, my_y], dest, row_off, flip))
    rhs_move = send(rhs_ref.at[:, half(other)], start_res.at[column(my_y), :], 0, True)
    for fact in facts:
        fact.wait_recv()

    def offset_of(row_of, listed_col):
        return float(3 * row_of * points - (listed_col - 1) * points)

    point_down = lax.broadcasted_iota(jnp.int32, (total, borrowed), 0).astype(jnp.float32)
    point_across = lax.broadcasted_iota(jnp.int32, (borrowed, total), 1).astype(jnp.float32)

    def hot(first, second):
        return jnp.where(first == second, 1.0, 0.0).astype(jnp.bfloat16)

    square_pad = jnp.zeros((borrowed - 8, borrowed), jnp.float32)
    for side in (0, -1, 1):
        place = row_of_side[side]
        for col in range(2):
            facts_here = info[place, col]
            row_ids = facts_here[3:4, :borrowed] - offset_of(1 - side, col)
            slots_here = pl.ds((2 * place + col) * borrowed, borrowed)
            put[:, slots_here] = hot(point_down, row_ids)
            turned = jnp.transpose(
                jnp.concatenate([facts_here[:, :borrowed], square_pad], axis=0)
            )
            pick[slots_here, :] = hot(turned[:, 3:4] - offset_of(1 - side, col), point_across)

    def parts_of(place):
        row = jnp.concatenate([info[place, 0], info[place, 1]], axis=1)
        return jnp.concatenate(
            [part.astype(jnp.float32) for part in split3(row)], axis=0
        ).astype(jnp.bfloat16)

    for col in range(2):
        ids = info[0, col][3:4, :borrowed]
        found = jnp.zeros((24, borrowed), jnp.float32)
        for side in (0, -1, 1):
            place = row_of_side[side]
            found = found + mm(parts_of(place), hot(point_down, ids - offset_of(1 + side, col)))
        found = found[0:8] + found[8:16] + found[16:24]
        row_shift = jnp.where(ids < 3.0 * points, -1.0, jnp.where(ids < 6.0 * points, 0.0, 1.0))
        within = ids - (row_shift + 1.0) * (3.0 * points)
        col_shift = jnp.where(within < points, -1.0, jnp.where(within < 2.0 * points, 0.0, 1.0))
        ext_here = jnp.concatenate(
            [found[0:1] + row_shift, found[1:2] + col_shift, found[2:3], found[3:8]], axis=0
        )
        ext_row[col] = ext_here
        ext_col[col] = jnp.transpose(jnp.concatenate([ext_here, square_pad], axis=0))
        for low_row in range(0, points, borrowed):
            part = info[0, col][:, low_row : low_row + borrowed]
            points_col[pl.ds(col * points + low_row, borrowed), :] = jnp.transpose(
                jnp.concatenate([part, square_pad], axis=0)
            )

    step = 32

    def own_diagonal(start, noise, width):
        here = lax.broadcasted_iota(jnp.int32, (step, width), 0) + start
        across = lax.broadcasted_iota(jnp.int32, (step, width), 1)
        return jnp.where(here == across, noise, 0.0)

    for col in range(2):

        def fill(index, carry, col=col):
            start = index * step
            rows = pl.ds(pl.multiple_of(col * points + start, step), step)
            local = pl.ds(pl.multiple_of(start, step), step)
            mine_x = points_col[rows, 0:1]
            mine_y = points_col[rows, 1:2]
            noise = points_col[rows, 2:3]
            for side in (0, -1, 1):
                place = row_of_side[side]
                for source in range(2):
                    there = info[place, source]
                    block = covariance(
                        mine_x,
                        mine_y,
                        there[0:1] + float(side),
                        there[1:2] + float(source - col),
                    )
                    if side == 0 and source == col:
                        block = block + own_diagonal(start, noise, points)
                        mats[col, local, 0:points] = block
                    cols = slice((2 * place + source) * points, (2 * place + source + 1) * points)
                    top[rows, cols], low[rows, cols] = split(block)
            mats[col, local, points:ext] = covariance(
                mine_x, mine_y, ext_row[col, 0:1], ext_row[col, 1:2]
            )
            return carry

        lax.fori_loop(0, points // step, fill, 0)

        def fill_ext(index, carry, col=col):
            start = index * step
            rows = pl.ds(pl.multiple_of(start, step), step)
            local = pl.ds(pl.multiple_of(points + start, step), step)
            mine_x = ext_col[col, rows, 0:1]
            mine_y = ext_col[col, rows, 1:2]
            noise = ext_col[col, rows, 2:3]
            mats[col, local, 0:points] = covariance(
                mine_x, mine_y, info[0, col, 0:1], info[0, col, 1:2]
            )
            block = covariance(mine_x, mine_y, ext_row[col, 0:1], ext_row[col, 1:2])
            mats[col, local, points:ext] = block + own_diagonal(start, noise, borrowed)
            return carry

        lax.fori_loop(0, borrowed // step, fill_ext, 0)

    def request(turn, value):
        both = wide(value)
        wanted = folded(mm(pick[...], both))
        own_asked[...] = wanted[: 2 * borrowed]
        moves = []
        for index, side in enumerate(SIDES):
            asked[turn, index] = wanted[2 * (index + 1) * borrowed : 2 * (index + 2) * borrowed]
            moves.append(send(asked.at[turn, index], got.at[turn, 1 - index], side))
        return both, moves

    def solve(turn, both, moves):
        for col in range(2):
            part = both[col * points : (col + 1) * points]
            accum_small[col] = mm(inv_top[col, :, :points], part) + mm(
                inv_low[col, :, :points], part
            )
        for move in moves:
            move.wait_recv()
        loaned = []
        for col in range(2):
            rows = slice(col * borrowed, (col + 1) * borrowed)
            loaned.append(wide(own_asked[rows] + got[turn, 0, rows] + got[turn, 1, rows]))
            tails[turn, rows] = folded(
                accum_small[col, points:]
                + mm(inv_top[col, points:, points:], loaned[col])
                + mm(inv_low[col, points:, points:], loaned[col])
            )
        returns = [
            send(tails.at[turn], back.at[turn, 1 - index], side)
            for index, side in enumerate(SIDES)
        ]
        owned = mm(put[:, : 2 * borrowed], wide(tails[turn]))
        for col in range(2):
            rows = slice(col * points, (col + 1) * points)
            basis[turn, rows] = folded(
                accum_small[col, :points]
                + mm(inv_top[col, :points, points:], loaned[col])
                + mm(inv_low[col, :points, points:], loaned[col])
                + owned[rows]
            )
        for move in returns:
            move.wait_recv()
        came = jnp.concatenate([wide(back[turn, 0]), wide(back[turn, 1])], axis=0)
        basis[turn] = basis[turn] + folded(mm(put[:, 2 * borrowed :], came))

    piece = total // CUTS

    def apply(turn):
        moves = []
        for cut in range(CUTS):
            rows = pl.ds(cut * piece, piece)
            for index, side in enumerate(SIDES):
                moves.append(
                    send(basis.at[turn, rows], window.at[turn, 1 - index, rows], side)
                )
        send_far(turn, basis)
        both = wide(basis[turn])
        accum[...] = mm(top[:, :total], both) + mm(low[:, :total], both)
        for cut in range(CUTS):
            for index in range(2):
                moves[2 * cut + index].wait_recv()
            for index in range(2):
                both = wide(window[turn, index, cut * piece : (cut + 1) * piece])
                cols = slice(
                    (index + 1) * total + cut * piece, (index + 1) * total + (cut + 1) * piece
                )
                accum[...] = accum[...] + (mm(top[:, cols], both) + mm(low[:, cols], both))
        images[turn] = folded(accum[...])

    far_moves = []

    def send_far(turn, source):
        index = turn if source is basis else ITERS + turn
        far_moves.append(send(source.at[turn, column(other)], far.at[index], 0, True))

    def begin_sum(turn, rows):
        mine[turn] = jnp.concatenate(rows, axis=0)
        index = counter[0]
        counter[0] += 1
        for hop in range(1, size_x):
            pltpu.make_async_remote_copy(
                src_ref=mine.at[turn],
                dst_ref=slots.at[turn, hop - 1],
                send_sem=send_sem.at[index],
                recv_sem=recv_sem.at[index],
                device_id={"gx": lax.rem(my_x + hop, size_x)},
                device_id_type=MESH,
            ).start()
        return index

    def end_sum(turn, index):
        held = slots.at[turn]
        pltpu.make_async_copy(held, held, recv_sem.at[index]).wait()
        pltpu.make_async_copy(held, held, send_sem.at[index]).wait()
        sums = mine[turn] + jnp.sum(slots[turn], axis=0)
        return sums[0:1], sums[1:2], sums[2:3]

    def inner(first, second):
        return jnp.sum(first * second, axis=0, keepdims=True)

    nothing = jnp.zeros((1, lanes), jnp.float32)

    rhs_move.wait_recv()
    asking = request(0, start_res[...])
    invert_both(mats)
    for col in range(2):
        inv_top[col], inv_low[col] = split(mats[col])
    solve(0, *asking)
    apply(0)
    send_far(0, images)
    summing = begin_sum(
        0, [inner(start_res[...], basis[0]), inner(basis[0], images[0]), nothing]
    )
    asking = request(1, images[0])
    solve(1, *asking)
    apply(1)
    send_far(1, images)
    gamma_0, curve_0, _ = end_sum(0, summing)
    alpha_0 = gamma_0 / curve_0
    work_image[...] = images[0] - alpha_0 * images[1]
    asking = request(2, work_image[...])
    work[...] = basis[0] - alpha_0 * basis[1]
    summing = begin_sum(
        1,
        [
            inner(start_res[...] - alpha_0 * images[0], work[...]),
            inner(work[...], work_image[...]),
            inner(work[...], images[0]),
        ],
    )
    solve(2, *asking)
    gamma_1, curve_1, mixed_1 = end_sum(1, summing)
    beta_1 = gamma_1 / gamma_0
    curve_1 = curve_1 + beta_1 * (2.0 * mixed_1 + beta_1 * curve_0)
    alpha_1 = gamma_1 / curve_1
    apply(2)
    send_far(2, images)
    old_image = work_image[...] + beta_1 * images[0]
    last = work[...] - alpha_1 * (basis[2] + beta_1 * basis[1])
    last_image = work_image[...] - alpha_1 * (images[2] + beta_1 * images[1])
    summing = begin_sum(
        2,
        [
            inner(start_res[...] - alpha_0 * images[0] - alpha_1 * old_image, last),
            inner(last, last_image),
            inner(last, old_image),
        ],
    )
    gamma_2, curve_2, mixed_2 = end_sum(2, summing)
    beta_2 = gamma_2 / gamma_1
    curve_2 = curve_2 + beta_2 * (2.0 * mixed_2 + beta_2 * curve_1)
    alpha_2 = gamma_2 / curve_2
    weights = [
        alpha_0 + alpha_1 * (1.0 + beta_1) + alpha_2 * (1.0 + beta_2 * (1.0 + beta_1)),
        -alpha_1 * alpha_0 - alpha_2 * (alpha_0 + alpha_1 * beta_1 + beta_2 * alpha_0),
        -alpha_2 * alpha_1,
    ]
    coef[...] = jnp.concatenate(weights + [jnp.zeros((5, lanes), jnp.float32)], axis=0)
    told = send(coef, far_coef, 0, True)
    held = column(my_y)
    solution_ref[:, half(my_y)] = (
        weights[0] * basis[0, held] + weights[1] * basis[1, held] + weights[2] * basis[2, held]
    )
    residual_ref[:, half(my_y)] = start_res[held, :] - (
        weights[0] * images[0, held] + weights[1] * images[1, held] + weights[2] * images[2, held]
    )
    for move in far_moves:
        move.wait_recv()
    told.wait_recv()
    weights = [far_coef[index : index + 1] for index in range(ITERS)]
    solution_ref[:, half(other)] = weights[0] * far[0] + weights[1] * far[1] + weights[2] * far[2]
    residual_ref[:, half(other)] = rhs_ref[:, half(other)] - (
        weights[0] * far[3] + weights[1] * far[4] + weights[2] * far[5]
    )
    for move in pending:
        move.wait_send()


def invert_both(mats):
    size = mats.shape[1]
    step = math.gcd(size, 128)
    rows = lax.broadcasted_iota(jnp.int32, (size, step), 0)
    lanes = lax.broadcasted_iota(jnp.int32, (size, step), 1)

    def eliminate(index, carry):
        start = pl.multiple_of(index * step, step)
        here = pl.ds(start, step)
        pivots = pivot_inverses([mats[which, here, here] for which in range(2)])
        inside = jnp.logical_and(rows >= start, rows < start + step)
        for which in range(2):
            column = jnp.where(inside, 0.0, mats[which, :, here])
            mats[which, :, here] = jnp.where(rows - start == lanes, 1.0, 0.0)
            row = full_dot(pivots[which], mats[which, here, :])
            mats[which] = mats[which] - full_dot(column, row)
            mats[which, here, :] = row
        return carry

    lax.fori_loop(0, size // step, eliminate, 0)


def paired_solve(right_side, coords, noise, intersect):
    points, width = right_side.shape
    size_x = lax.axis_size("gx")
    borrowed = intersect.shape[1]
    lanes, total, ext = width // 2, 2 * points, points + borrowed
    moves = 5 + 1 + ITERS * (2 + 2 + 2 * CUTS + 2 + 1) + 1
    out = jax.ShapeDtypeStruct(right_side.shape, jnp.float32)
    f32 = lambda *shape: pltpu.VMEM(shape, jnp.float32)
    b16 = lambda *shape: pltpu.VMEM(shape, jnp.bfloat16)
    return pl.pallas_call(
        paired_kernel,
        out_shape=(out, out),
        in_specs=[VMEM] * 4,
        out_specs=(VMEM, VMEM),
        scratch_shapes=[
            f32(3, 2, 8, points),
            f32(total, borrowed),
            f32(2, 8, borrowed),
            f32(2, borrowed, borrowed),
            b16(total, 3 * total),
            b16(total, 3 * total),
            f32(2, ext, ext),
            b16(2, ext, ext),
            b16(2, ext, ext),
            b16(6 * borrowed, total),
            b16(total, 6 * borrowed),
            f32(total, lanes),
            f32(ITERS, total, lanes),
            f32(ITERS, total, lanes),
            f32(total, lanes),
            f32(total, lanes),
            f32(total, 2 * lanes),
            f32(2, ext, 2 * lanes),
            f32(ITERS, 2, 2 * borrowed, lanes),
            f32(2 * borrowed, lanes),
            f32(ITERS, 2, 2 * borrowed, lanes),
            f32(ITERS, 2 * borrowed, lanes),
            f32(ITERS, 2, 2 * borrowed, lanes),
            f32(ITERS, 2, total, lanes),
            f32(2 * ITERS, points, lanes),
            f32(ITERS, 3, lanes),
            f32(ITERS, size_x - 1, 3, lanes),
            f32(8, lanes),
            f32(8, lanes),
            pltpu.SemaphoreType.DMA((moves,)),
            pltpu.SemaphoreType.DMA((moves,)),
        ],
        compiler_params=pltpu.CompilerParams(
            collective_id=0, has_side_effects=True, vmem_limit_bytes=58 * 1024 * 1024
        ),
    )(right_side, coords, noise, intersect)


def paired_shards(right_side, coords, noise, intersect):
    points, width = right_side.shape[2:]
    answer, residual = paired_solve(
        right_side.reshape(points, width),
        coords.reshape(2, points),
        noise.reshape(1, points),
        intersect.reshape(1, intersect.shape[2]),
    )
    return answer.reshape(right_side.shape), residual.reshape(right_side.shape)


def solution(mesh):
    placed = (
        P("gx", "gy", None, None),
        P("gx", "gy", None, None),
        P("gx", "gy", None),
        P("gx", "gy", None),
    )
    return jax.shard_map(
        paired_shards if mesh.shape["gy"] == 2 else shards,
        mesh=mesh,
        in_specs=placed,
        out_specs=(P("gx", "gy", None, None), P("gx", "gy", None, None)),
        check_vma=False,
    )
```

profile of v0, /device:TPU:0, one launch (start us, length us, event | category | flops | bytes accessed | tf_op | source)
XLA Modules:
  0.0 137.7 jit_solution(798772190208714308)
XLA Ops:
  0.6 134.3 %shard_map.59 = (f32[512,256]{1,0:T(8,128)}, f32[512,256]{1,0:T(8,128)}) custom-call(f32[512,256]{1,0:T(8,128)} %bitcast.6, f32[2,512]{1,0:T(2,128)} %bitcast.9, f32[1,512]{1,0:T(1,128)} %bitcast.10, s32[1,128]{1,0:T(1,128)} %bitcast.11), custom_call_target="tpu_custom_call" | custom-call | tf_op jit(solution)/shard_map/pallas_call | solution.py:961
  135.0 0.0 copy-start
  135.0 1.9 %copy.8 = f32[1,1,512,256]{3,2,1,0:T(8,128)} copy(f32[1,1,512,256]{3,2,1,0:T(8,128)} %bitcast.8) | data formatting | bytes 1048576
  136.9 0.0 copy-done
  136.9 0.8 copy.9
Async XLA Ops:
  135.0 1.9 %copy-start = (f32[512,256]{1,0:T(8,128)S(1)}, f32[512,256]{1,0:T(8,128)}, u32[]{:S(2)}) copy-start(f32[512,256]{1,0:T(8,128)} %get-tuple-element.5) | copy-start | bytes 1572868
where the time goes:
time: 138 us
  Pallas kernels  134 us (97%)
  local copies, waits for them, and re-layouts  2.72 us (2%)
    pallas_call x1, Pallas kernels, paired_solve(): pl.pallas_call(paired_kernel, out_shape=(out, out), in_specs=[VMEM] * 4,...  134 us

commit v1 on v0

--- a/solution.py
+++ b/solution.py
@@ -527,7 +527,7 @@
     return (1.0 + scaled) * jnp.exp(-scaled) * taper
 
 
-def pivot_inverses(blocks):
+def pivot_inverses(blocks, between=lambda: None):
     size = blocks[0].shape[0]
     low, high = NOISE_MIN * 0.97, (size + 1.0) * 1.01
     eye = (
@@ -540,6 +540,7 @@
     scale = 2.0 / (2.0 - gap * gap)
     guesses = [(scale * first) * (eye + rest) for rest in rests]
     rests = [scale * full_dot(rest, rest) + (1.0 - scale) * eye for rest in rests]
+    between()
     gap = gap * gap / (2.0 - gap * gap)
     while True:
         scale = 2.0 / (2.0 - gap * gap)
@@ -548,6 +549,7 @@
             guesses = [
                 scale * (guess + full_dot(rest, guess)) for rest, guess in zip(rests, guesses)
             ]
+            between()
             break
         both = [
             full_dot(rest, jnp.concatenate([rest, guess], axis=1))
@@ -555,9 +557,12 @@
         ]
         guesses = [scale * (guess + pair[:, size:]) for guess, pair in zip(guesses, both)]
         rests = [scale * pair[:, :size] + (1.0 - scale) * eye for pair in both]
+        between()
     for _ in range(2):
         errors = [eye - full_dot(block, guess) for block, guess in zip(blocks, guesses)]
+        between()
         guesses = [guess + dot3(guess, error) for guess, error in zip(guesses, errors)]
+        between()
     return guesses
 
 
@@ -569,8 +574,8 @@
     rhs_ref, coords_ref, noise_ref, ids_ref,
     solution_ref, residual_ref,
     info, points_col, ext_row, ext_col, top, low, mats, inv_top, inv_low, pick, put,
-    start_res, basis, images, work, work_image, accum, accum_small,
-    asked, own_asked, got, tails, back, window, far, mine, slots, coef, far_coef,
+    start_res, basis, images, work, work_image, last, old_image, accum, accum_small,
+    asked, own_asked, got, tails, back, window, far, mine, slots, pivots, crossing,
     send_sem, recv_sem,
 ):
     size_x, size_y = lax.axis_size("gx"), lax.axis_size("gy")
@@ -613,12 +618,9 @@
     column = lambda which: pl.ds(pl.multiple_of(which * points, points), points)
 
     barrier = pltpu.get_barrier_semaphore()
-    for hop in range(1, size_x):
-        pl.semaphore_signal(
-            barrier, inc=1, device_id={"gx": lax.rem(my_x + hop, size_x)}, device_id_type=MESH
-        )
-    for row_off in (0, -1, 1):
-        pl.semaphore_signal(barrier, inc=1, device_id=near(row_off, True), device_id_type=MESH)
+    peers = [(hop, False) for hop in range(1, size_x)] + [(hop, True) for hop in range(size_x)]
+    for hop, flip in peers:
+        pl.semaphore_signal(barrier, inc=1, device_id=near(hop, flip), device_id_type=MESH)
 
     info[0, my_y] = jnp.concatenate(
         [
@@ -636,7 +638,7 @@
         axis=0,
     )
     start_res[column(my_y), :] = rhs_ref[:, half(my_y)]
-    pl.semaphore_wait(barrier, size_x - 1 + 3)
+    pl.semaphore_wait(barrier, len(peers))
 
     facts = []
     for row_off, flip in ((0, True), (-1, False), (1, False), (-1, True), (1, True)):
@@ -702,36 +704,56 @@
         across = lax.broadcasted_iota(jnp.int32, (step, width), 1)
         return jnp.where(here == across, noise, 0.0)
 
+    def block_of(rows, col, side, source):
+        there = info[row_of_side[side], source]
+        return covariance(
+            points_col[rows, 0:1],
+            points_col[rows, 1:2],
+            there[0:1] + float(side),
+            there[1:2] + float(source - col),
+        )
+
+    def cols_of(side, source):
+        at = (2 * row_of_side[side] + source) * points
+        return slice(at, at + points)
+
+    def fill(pairs, rows_step):
+        for col in range(2):
+
+            def some(index, carry, col=col):
+                start = pl.multiple_of(col * points + index * rows_step, rows_step)
+                rows = pl.ds(start, rows_step)
+                for side, source in pairs(col):
+                    cols = cols_of(side, source)
+                    top[rows, cols], low[rows, cols] = split(block_of(rows, col, side, source))
+                return carry
+
+            lax.fori_loop(0, points // rows_step, some, 0)
+
+    def fill_cross():
+        fill(lambda col: [(0, 1 - col)], 32)
+
+    def fill_sides():
+        fill(lambda col: [(side, source) for side in SIDES for source in range(2)], 32)
+
     for col in range(2):
 
-        def fill(index, carry, col=col):
+        def fill_own(index, carry, col=col):
             start = index * step
             rows = pl.ds(pl.multiple_of(col * points + start, step), step)
             local = pl.ds(pl.multiple_of(start, step), step)
-            mine_x = points_col[rows, 0:1]
-            mine_y = points_col[rows, 1:2]
-            noise = points_col[rows, 2:3]
-            for side in (0, -1, 1):
-                place = row_of_side[side]
-                for source in range(2):
-                    there = info[place, source]
-                    block = covariance(
-                        mine_x,
-                        mine_y,
-                        there[0:1] + float(side),
-                        there[1:2] + float(source - col),
-                    )
-                    if side == 0 and source == col:
-                        block = block + own_diagonal(start, noise, points)
-                        mats[col, local, 0:points] = block
-                    cols = slice((2 * place + source) * points, (2 * place + source + 1) * points)
-                    top[rows, cols], low[rows, cols] = split(block)
+            block = block_of(rows, col, 0, col)
+            block = block + own_diagonal(start, points_col[rows, 2:3], points)
+            mats[col, local, 0:points] = block
+            cols = cols_of(0, col)
+            top[rows, cols], low[rows, cols] = split(block)
             mats[col, local, points:ext] = covariance(
-                mine_x, mine_y, ext_row[col, 0:1], ext_row[col, 1:2]
+                points_col[rows, 0:1], points_col[rows, 1:2],
+                ext_row[col, 0:1], ext_row[col, 1:2],
             )
             return carry
 
-        lax.fori_loop(0, points // step, fill, 0)
+        lax.fori_loop(0, points // step, fill_own, 0)
 
         def fill_ext(index, carry, col=col):
             start = index * step
@@ -749,6 +771,11 @@
 
         lax.fori_loop(0, borrowed // step, fill_ext, 0)
 
+    def joined(first, second, both):
+        return mm(
+            jnp.concatenate([first, second], axis=1), jnp.concatenate([both, both], axis=0)
+        )
+
     def request(turn, value):
         both = wide(value)
         wanted = folded(mm(pick[...], both))
@@ -759,12 +786,10 @@
             moves.append(send(asked.at[turn, index], got.at[turn, 1 - index], side))
         return both, moves
 
-    def solve(turn, both, moves):
+    def solve(turn, both, moves, meanwhile=lambda: None):
         for col in range(2):
             part = both[col * points : (col + 1) * points]
-            accum_small[col] = mm(inv_top[col, :, :points], part) + mm(
-                inv_low[col, :, :points], part
-            )
+            accum_small[col] = joined(inv_top[col, :, :points], inv_low[col, :, :points], part)
         for move in moves:
             move.wait_recv()
         loaned = []
@@ -773,8 +798,7 @@
             loaned.append(wide(own_asked[rows] + got[turn, 0, rows] + got[turn, 1, rows]))
             tails[turn, rows] = folded(
                 accum_small[col, points:]
-                + mm(inv_top[col, points:, points:], loaned[col])
-                + mm(inv_low[col, points:, points:], loaned[col])
+                + joined(inv_top[col, points:, points:], inv_low[col, points:, points:], loaned[col])
             )
         returns = [
             send(tails.at[turn], back.at[turn, 1 - index], side)
@@ -785,37 +809,42 @@
             rows = slice(col * points, (col + 1) * points)
             basis[turn, rows] = folded(
                 accum_small[col, :points]
-                + mm(inv_top[col, :points, points:], loaned[col])
-                + mm(inv_low[col, :points, points:], loaned[col])
+                + joined(inv_top[col, :points, points:], inv_low[col, :points, points:], loaned[col])
                 + owned[rows]
             )
+        meanwhile()
         for move in returns:
             move.wait_recv()
         came = jnp.concatenate([wide(back[turn, 0]), wide(back[turn, 1])], axis=0)
         basis[turn] = basis[turn] + folded(mm(put[:, 2 * borrowed :], came))
 
     piece = total // CUTS
-
-    def apply(turn):
-        moves = []
+    close = 1 - lax.rem(my_x, 2)
+
+    def apply(turn, meanwhile=lambda: None):
+        first = counter[0]
         for cut in range(CUTS):
             rows = pl.ds(cut * piece, piece)
             for index, side in enumerate(SIDES):
-                moves.append(
-                    send(basis.at[turn, rows], window.at[turn, 1 - index, rows], side)
-                )
+                send(basis.at[turn, rows], window.at[turn, 1 - index, rows], side)
         send_far(turn, basis)
-        both = wide(basis[turn])
-        accum[...] = mm(top[:, :total], both) + mm(low[:, :total], both)
+
+        def landed(cut, index):
+            place = window.at[turn, index, pl.ds(cut * piece, piece)]
+            semaphore = recv_sem.at[first + 2 * cut + 1 - index]
+            pltpu.make_async_copy(place, place, semaphore).wait()
+
+        accum[...] = joined(top[:, :total], low[:, :total], wide(basis[turn]))
+        meanwhile()
         for cut in range(CUTS):
-            for index in range(2):
-                moves[2 * cut + index].wait_recv()
-            for index in range(2):
-                both = wide(window[turn, index, cut * piece : (cut + 1) * piece])
-                cols = slice(
-                    (index + 1) * total + cut * piece, (index + 1) * total + (cut + 1) * piece
-                )
-                accum[...] = accum[...] + (mm(top[:, cols], both) + mm(low[:, cols], both))
+            landed(cut, close)
+        cols = pl.ds(pl.multiple_of((close + 1) * total, total), total)
+        accum[...] = accum[...] + joined(top[:, cols], low[:, cols], wide(window[turn, close]))
+        for cut in range(CUTS):
+            landed(cut, 1 - close)
+            both = wide(window[turn, 1 - close, cut * piece : (cut + 1) * piece])
+            cols = pl.ds(pl.multiple_of((2 - close) * total + cut * piece, piece), piece)
+            accum[...] = accum[...] + joined(top[:, cols], low[:, cols], both)
         images[turn] = folded(accum[...])
 
     far_moves = []
@@ -828,13 +857,13 @@
         mine[turn] = jnp.concatenate(rows, axis=0)
         index = counter[0]
         counter[0] += 1
-        for hop in range(1, size_x):
+        for place, (hop, flip) in enumerate(peers):
             pltpu.make_async_remote_copy(
                 src_ref=mine.at[turn],
-                dst_ref=slots.at[turn, hop - 1],
+                dst_ref=slots.at[turn, place],
                 send_sem=send_sem.at[index],
                 recv_sem=recv_sem.at[index],
-                device_id={"gx": lax.rem(my_x + hop, size_x)},
+                device_id=near(hop, flip),
                 device_id_type=MESH,
             ).start()
         return index
@@ -843,8 +872,15 @@
         held = slots.at[turn]
         pltpu.make_async_copy(held, held, recv_sem.at[index]).wait()
         pltpu.make_async_copy(held, held, send_sem.at[index]).wait()
-        sums = mine[turn] + jnp.sum(slots[turn], axis=0)
-        return sums[0:1], sums[1:2], sums[2:3]
+        here = mine[turn] + jnp.sum(slots[turn, : size_x - 1], axis=0)
+        there = jnp.sum(slots[turn, size_x - 1 :], axis=0)
+        return [(here[row : row + 1], there[row : row + 1]) for row in range(3)]
+
+    def over(first, second):
+        return tuple(a / b for a, b in zip(first, second))
+
+    def curve_of(curved, mixed, ratio, old):
+        return tuple(c + b * (2.0 * m + b * o) for c, m, b, o in zip(curved, mixed, ratio, old))
 
     def inner(first, second):
         return jnp.sum(first * second, axis=0, keepdims=True)
@@ -853,11 +889,11 @@
 
     rhs_move.wait_recv()
     asking = request(0, start_res[...])
-    invert_both(mats)
+    invert_both(mats, pivots, crossing)
     for col in range(2):
         inv_top[col], inv_low[col] = split(mats[col])
-    solve(0, *asking)
-    apply(0)
+    solve(0, *asking, fill_cross)
+    apply(0, fill_sides)
     send_far(0, images)
     summing = begin_sum(
         0, [inner(start_res[...], basis[0]), inner(basis[0], images[0]), nothing]
@@ -867,47 +903,59 @@
     apply(1)
     send_far(1, images)
     gamma_0, curve_0, _ = end_sum(0, summing)
-    alpha_0 = gamma_0 / curve_0
-    work_image[...] = images[0] - alpha_0 * images[1]
+    alpha_0 = over(gamma_0, curve_0)
+    step_0 = alpha_0[0]
+    work_image[...] = images[0] - step_0 * images[1]
     asking = request(2, work_image[...])
-    work[...] = basis[0] - alpha_0 * basis[1]
+    work[...] = basis[0] - step_0 * basis[1]
     summing = begin_sum(
         1,
         [
-            inner(start_res[...] - alpha_0 * images[0], work[...]),
+            inner(start_res[...] - step_0 * images[0], work[...]),
             inner(work[...], work_image[...]),
             inner(work[...], images[0]),
         ],
     )
     solve(2, *asking)
     gamma_1, curve_1, mixed_1 = end_sum(1, summing)
-    beta_1 = gamma_1 / gamma_0
-    curve_1 = curve_1 + beta_1 * (2.0 * mixed_1 + beta_1 * curve_0)
-    alpha_1 = gamma_1 / curve_1
-    apply(2)
+    beta_1 = over(gamma_1, gamma_0)
+    curve_1 = curve_of(curve_1, mixed_1, beta_1, curve_0)
+    alpha_1 = over(gamma_1, curve_1)
+    step_1, ratio_1 = alpha_1[0], beta_1[0]
+
+    def prepare():
+        old_image[...] = work_image[...] + ratio_1 * images[0]
+        last[...] = work[...] - step_1 * (basis[2] + ratio_1 * basis[1])
+        work_image[...] = work_image[...] - (step_1 * ratio_1) * images[1]
+
+    apply(2, prepare)
     send_far(2, images)
-    old_image = work_image[...] + beta_1 * images[0]
-    last = work[...] - alpha_1 * (basis[2] + beta_1 * basis[1])
-    last_image = work_image[...] - alpha_1 * (images[2] + beta_1 * images[1])
+    last_image = work_image[...] - step_1 * images[2]
     summing = begin_sum(
         2,
         [
-            inner(start_res[...] - alpha_0 * images[0] - alpha_1 * old_image, last),
-            inner(last, last_image),
-            inner(last, old_image),
+            inner(
+                start_res[...] - step_0 * images[0] - step_1 * old_image[...], last[...]
+            ),
+            inner(last[...], last_image),
+            inner(last[...], old_image[...]),
         ],
     )
     gamma_2, curve_2, mixed_2 = end_sum(2, summing)
-    beta_2 = gamma_2 / gamma_1
-    curve_2 = curve_2 + beta_2 * (2.0 * mixed_2 + beta_2 * curve_1)
-    alpha_2 = gamma_2 / curve_2
-    weights = [
-        alpha_0 + alpha_1 * (1.0 + beta_1) + alpha_2 * (1.0 + beta_2 * (1.0 + beta_1)),
-        -alpha_1 * alpha_0 - alpha_2 * (alpha_0 + alpha_1 * beta_1 + beta_2 * alpha_0),
-        -alpha_2 * alpha_1,
-    ]
-    coef[...] = jnp.concatenate(weights + [jnp.zeros((5, lanes), jnp.float32)], axis=0)
-    told = send(coef, far_coef, 0, True)
+    beta_2 = over(gamma_2, gamma_1)
+    curve_2 = curve_of(curve_2, mixed_2, beta_2, curve_1)
+    alpha_2 = over(gamma_2, curve_2)
+
+    def weights_of(half_at):
+        a_0, a_1, a_2 = alpha_0[half_at], alpha_1[half_at], alpha_2[half_at]
+        b_1, b_2 = beta_1[half_at], beta_2[half_at]
+        return (
+            a_0 + a_1 * (1.0 + b_1) + a_2 * (1.0 + b_2 * (1.0 + b_1)),
+            -a_1 * a_0 - a_2 * (a_0 + a_1 * b_1 + b_2 * a_0),
+            -a_2 * a_1,
+        )
+
+    weights = weights_of(0)
     held = column(my_y)
     solution_ref[:, half(my_y)] = (
         weights[0] * basis[0, held] + weights[1] * basis[1, held] + weights[2] * basis[2, held]
@@ -917,8 +965,7 @@
     )
     for move in far_moves:
         move.wait_recv()
-    told.wait_recv()
-    weights = [far_coef[index : index + 1] for index in range(ITERS)]
+    weights = weights_of(1)
     solution_ref[:, half(other)] = weights[0] * far[0] + weights[1] * far[1] + weights[2] * far[2]
     residual_ref[:, half(other)] = rhs_ref[:, half(other)] - (
         weights[0] * far[3] + weights[1] * far[4] + weights[2] * far[5]
@@ -927,26 +974,55 @@
         move.wait_send()
 
 
-def invert_both(mats):
-    size = mats.shape[1]
-    step = math.gcd(size, 128)
+def invert_both(mats, pivots, crossing):
+    size, step = mats.shape[1], pivots.shape[1]
     rows = lax.broadcasted_iota(jnp.int32, (size, step), 0)
     lanes = lax.broadcasted_iota(jnp.int32, (size, step), 1)
 
-    def eliminate(index, carry):
+    def eliminate(index, ahead):
         start = pl.multiple_of(index * step, step)
         here = pl.ds(start, step)
-        pivots = pivot_inverses([mats[which, here, here] for which in range(2)])
         inside = jnp.logical_and(rows >= start, rows < start + step)
+        columns, pivot_rows = [], []
         for which in range(2):
-            column = jnp.where(inside, 0.0, mats[which, :, here])
+            columns.append(jnp.where(inside, 0.0, mats[which, :, here]))
             mats[which, :, here] = jnp.where(rows - start == lanes, 1.0, 0.0)
-            row = full_dot(pivots[which], mats[which, here, :])
-            mats[which] = mats[which] - full_dot(column, row)
-            mats[which, here, :] = row
+            pivot_rows.append(full_dot(pivots[which], mats[which, here, :]))
+            mats[which, here, :] = pivot_rows[which]
+
+        def update(which, low):
+            part = slice(low, low + step)
+            mats[which, part, :] = mats[which, part, :] - full_dot(
+                columns[which][part], pivot_rows[which]
+            )
+
+        left = [(which, low) for low in range(0, size, step) for which in range(2)]
+        if ahead:
+            there = pl.ds(pl.multiple_of(start + step, step), step)
+            blocks = []
+            for which in range(2):
+                crossing[which] = columns[which]
+                blocks.append(
+                    mats[which, there, there]
+                    - full_dot(crossing[which, there, :], mats[which, here, there])
+                )
+            found = pivot_inverses(blocks, lambda: left and update(*left.pop(0)))
+        while left:
+            update(*left.pop(0))
+        for which in range(2):
+            mats[which, here, :] = pivot_rows[which]
+            if ahead:
+                pivots[which] = found[which]
+
+    def looped(index, carry):
+        eliminate(index, True)
         return carry
 
-    lax.fori_loop(0, size // step, eliminate, 0)
+    first = slice(0, step)
+    for which, pivot in enumerate(pivot_inverses([mats[at, first, first] for at in range(2)])):
+        pivots[which] = pivot
+    lax.fori_loop(0, size // step - 1, looped, 0)
+    eliminate(size // step - 1, False)
 
 
 def paired_solve(right_side, coords, noise, intersect):
@@ -954,7 +1030,7 @@
     size_x = lax.axis_size("gx")
     borrowed = intersect.shape[1]
     lanes, total, ext = width // 2, 2 * points, points + borrowed
-    moves = 5 + 1 + ITERS * (2 + 2 + 2 * CUTS + 2 + 1) + 1
+    moves = 5 + 1 + ITERS * (2 + 2 + 2 * CUTS + 2 + 1)
     out = jax.ShapeDtypeStruct(right_side.shape, jnp.float32)
     f32 = lambda *shape: pltpu.VMEM(shape, jnp.float32)
     b16 = lambda *shape: pltpu.VMEM(shape, jnp.bfloat16)
@@ -980,6 +1056,8 @@
             f32(ITERS, total, lanes),
             f32(total, lanes),
             f32(total, lanes),
+            f32(total, lanes),
+            f32(total, lanes),
             f32(total, 2 * lanes),
             f32(2, ext, 2 * lanes),
             f32(ITERS, 2, 2 * borrowed, lanes),
@@ -990,9 +1068,9 @@
             f32(ITERS, 2, total, lanes),
             f32(2 * ITERS, points, lanes),
             f32(ITERS, 3, lanes),
-            f32(ITERS, size_x - 1, 3, lanes),
-            f32(8, lanes),
-            f32(8, lanes),
+            f32(ITERS, 2 * size_x - 1, 3, lanes),
+            f32(2, borrowed, borrowed),
+            f32(2, ext, borrowed),
             pltpu.SemaphoreType.DMA((moves,)),
             pltpu.SemaphoreType.DMA((moves,)),
         ],

time: 138 us -> 124 us (0.90)
  Pallas kernels: 134 us -> 120 us
    pallas_call x1, Pallas kernels: 134 us -> 120 us  [paired_solve(): pl.pallas_call(paired_kernel, out_shape=(out, out), in_specs=[VMEM] * 4,...]
where the time goes in v1:
time: 124 us; the launch traced here: 123 us
  Pallas kernels  120 us (97%)
  local copies, waits for them, and re-layouts  2.72 us (2%)
    pallas_call x1, Pallas kernels, paired_solve(): pl.pallas_call(paired_kernel, out_shape=(out, out), in_specs=[VMEM] * 4,...  120 us
    unnamed x4, local copies, waits for them, and re-layouts  2.72 us

profile of v1, /device:TPU:0, one launch (start us, length us, event | category | flops | bytes accessed | tf_op | source)
XLA Modules:
  0.0 123.5 jit_solution(8595489304428128413)
XLA Ops:
  0.6 120.1 %shard_map.59 = (f32[512,256]{1,0:T(8,128)}, f32[512,256]{1,0:T(8,128)}) custom-call(f32[512,256]{1,0:T(8,128)} %bitcast.6, f32[2,512]{1,0:T(2,128)} %bitcast.9, f32[1,512]{1,0:T(1,128)} %bitcast.10, s32[1,128]{1,0:T(1,128)} %bitcast.11), custom_call_target="tpu_custom_call" | custom-call | tf_op jit(solution)/shard_map/pallas_call | solution.py:1037
  120.7 0.0 copy-start
  120.8 1.9 %copy.8 = f32[1,1,512,256]{3,2,1,0:T(8,128)} copy(f32[1,1,512,256]{3,2,1,0:T(8,128)} %bitcast.8) | data formatting | bytes 1048576
  122.7 0.0 copy-done
  122.7 0.8 copy.9
Async XLA Ops:
  120.7 1.9 %copy-start = (f32[512,256]{1,0:T(8,128)S(1)}, f32[512,256]{1,0:T(8,128)}, u32[]{:S(2)}) copy-start(f32[512,256]{1,0:T(8,128)} %get-tuple-element.5) | copy-start | bytes 1572868

commit v2 on v1

--- a/solution.py
+++ b/solution.py
@@ -516,15 +516,15 @@
 
 
 def covariance(rows_x, rows_y, cols_x, cols_y):
-    delta_x = rows_x - cols_x
-    delta_y = rows_y - cols_y
+    rate = ROOT_THREE / RANGE_LEN
+    delta_x = rate * rows_x - rate * cols_x
+    delta_y = rate * rows_y - rate * cols_y
     square = delta_x * delta_x + delta_y * delta_y
-    distance = square * lax.rsqrt(jnp.maximum(square, 1e-30))
-    scaled = ROOT_THREE / RANGE_LEN * distance
-    rest = 1.0 - jnp.minimum(distance, 1.0)
+    scaled = square * lax.rsqrt(jnp.maximum(square, 1e-30))
+    rest = jnp.maximum(1.0 - (1.0 / rate) * scaled, 0.0)
     rest = rest * rest
-    taper = rest * rest * (4.0 * jnp.minimum(distance, 1.0) + 1.0)
-    return (1.0 + scaled) * jnp.exp(-scaled) * taper
+    shape = 1.0 + scaled * ((1.0 + 4.0 / rate) + (4.0 / rate) * scaled)
+    return shape * jnp.exp(-scaled) * (rest * rest)
 
 
 def pivot_inverses(blocks, between=lambda: None):
@@ -539,7 +539,7 @@
     rests = [eye - first * block for block in blocks]
     scale = 2.0 / (2.0 - gap * gap)
     guesses = [(scale * first) * (eye + rest) for rest in rests]
-    rests = [scale * full_dot(rest, rest) + (1.0 - scale) * eye for rest in rests]
+    rests = [scale * dot3(rest, rest) + (1.0 - scale) * eye for rest in rests]
     between()
     gap = gap * gap / (2.0 - gap * gap)
     while True:
@@ -547,23 +547,20 @@
         gap = gap * gap / (2.0 - gap * gap)
         if gap < 1e-3:
             guesses = [
-                scale * (guess + full_dot(rest, guess)) for rest, guess in zip(rests, guesses)
+                scale * (guess + dot3(rest, guess)) for rest, guess in zip(rests, guesses)
             ]
             between()
             break
         both = [
-            full_dot(rest, jnp.concatenate([rest, guess], axis=1))
+            dot3(rest, jnp.concatenate([rest, guess], axis=1))
             for rest, guess in zip(rests, guesses)
         ]
         guesses = [scale * (guess + pair[:, size:]) for guess, pair in zip(guesses, both)]
         rests = [scale * pair[:, :size] + (1.0 - scale) * eye for pair in both]
         between()
-    for _ in range(2):
-        errors = [eye - full_dot(block, guess) for block, guess in zip(blocks, guesses)]
-        between()
-        guesses = [guess + dot3(guess, error) for guess, error in zip(guesses, errors)]
-        between()
-    return guesses
+    errors = [eye - full_dot(block, guess) for block, guess in zip(blocks, guesses)]
+    between()
+    return [guess + dot3(guess, error) for guess, error in zip(guesses, errors)]
 
 
 SIDES = (-1, 1)
@@ -571,9 +568,9 @@
 
 
 def paired_kernel(
-    rhs_ref, coords_ref, noise_ref, ids_ref,
+    rhs_hbm, coords_ref, noise_ref, ids_ref,
     solution_ref, residual_ref,
-    info, points_col, ext_row, ext_col, top, low, mats, inv_top, inv_low, pick, put,
+    rhs_ref, rhs_sem, info, points_col, ext_row, ext_col, top, low, mats, inv_top, inv_low, pick, put,
     start_res, basis, images, work, work_image, last, old_image, accum, accum_small,
     asked, own_asked, got, tails, back, window, far, mine, slots, pivots, crossing,
     send_sem, recv_sem,
@@ -593,7 +590,7 @@
 
     def near(row_off, flip):
         place = {}
-        if row_off:
+        if not isinstance(row_off, int) or row_off:
             place["gx"] = lax.rem(my_x + row_off + size_x, size_x)
         if flip:
             place["gy"] = other
@@ -617,6 +614,8 @@
     half = lambda which: pl.ds(pl.multiple_of(which * lanes, lanes), lanes)
     column = lambda which: pl.ds(pl.multiple_of(which * points, points), points)
 
+    loading = pltpu.make_async_copy(rhs_hbm, rhs_ref, rhs_sem)
+    loading.start()
     barrier = pltpu.get_barrier_semaphore()
     peers = [(hop, False) for hop in range(1, size_x)] + [(hop, True) for hop in range(size_x)]
     for hop, flip in peers:
@@ -637,14 +636,48 @@
         ],
         axis=0,
     )
-    start_res[column(my_y), :] = rhs_ref[:, half(my_y)]
     pl.semaphore_wait(barrier, len(peers))
 
     facts = []
     for row_off, flip in ((0, True), (-1, False), (1, False), (-1, True), (1, True)):
         dest = info.at[row_of_side[-row_off], my_y]
         facts.append(send(info.at[0, my_y], dest, row_off, flip))
+    loading.wait()
     rhs_move = send(rhs_ref.at[:, half(other)], start_res.at[column(my_y), :], 0, True)
+    start_res[column(my_y), :] = rhs_ref[:, half(my_y)]
+
+    square_pad = jnp.zeros((borrowed - 8, borrowed), jnp.float32)
+    step = 64
+
+    def own_diagonal(start, noise, width):
+        here = lax.broadcasted_iota(jnp.int32, (noise.shape[0], width), 0) + start
+        across = lax.broadcasted_iota(jnp.int32, (noise.shape[0], width), 1)
+        return jnp.where(here == across, noise, 0.0)
+
+    def fill_own(which):
+        for low_row in range(0, points, borrowed):
+            part = info[0, which][:, low_row : low_row + borrowed]
+            rows = pl.ds(pl.multiple_of(which * points + low_row, borrowed), borrowed)
+            points_col[rows, :] = jnp.transpose(jnp.concatenate([part, square_pad], axis=0))
+
+        def some(index, carry):
+            start = index * step
+            rows = pl.ds(pl.multiple_of(which * points + start, step), step)
+            block = covariance(
+                points_col[rows, 0:1],
+                points_col[rows, 1:2],
+                info[0, which, 0:1],
+                info[0, which, 1:2],
+            )
+            block = block + own_diagonal(start, points_col[rows, 2:3], points)
+            mats[which, pl.ds(pl.multiple_of(start, step), step), 0:points] = block
+            cols = column(which)
+            top[rows, cols], low[rows, cols] = split(block)
+            return carry
+
+        lax.fori_loop(0, points // step, some, 0)
+
+    fill_own(my_y)
     for fact in facts:
         fact.wait_recv()
 
@@ -657,7 +690,6 @@
     def hot(first, second):
         return jnp.where(first == second, 1.0, 0.0).astype(jnp.bfloat16)
 
-    square_pad = jnp.zeros((borrowed - 8, borrowed), jnp.float32)
     for side in (0, -1, 1):
         place = row_of_side[side]
         for col in range(2):
@@ -691,18 +723,6 @@
         )
         ext_row[col] = ext_here
         ext_col[col] = jnp.transpose(jnp.concatenate([ext_here, square_pad], axis=0))
-        for low_row in range(0, points, borrowed):
-            part = info[0, col][:, low_row : low_row + borrowed]
-            points_col[pl.ds(col * points + low_row, borrowed), :] = jnp.transpose(
-                jnp.concatenate([part, square_pad], axis=0)
-            )
-
-    step = 32
-
-    def own_diagonal(start, noise, width):
-        here = lax.broadcasted_iota(jnp.int32, (step, width), 0) + start
-        across = lax.broadcasted_iota(jnp.int32, (step, width), 1)
-        return jnp.where(here == across, noise, 0.0)
 
     def block_of(rows, col, side, source):
         there = info[row_of_side[side], source]
@@ -731,29 +751,13 @@
             lax.fori_loop(0, points // rows_step, some, 0)
 
     def fill_cross():
-        fill(lambda col: [(0, 1 - col)], 32)
+        fill(lambda col: [(0, 1 - col)], 64)
 
     def fill_sides():
         fill(lambda col: [(side, source) for side in SIDES for source in range(2)], 32)
 
+    fill_own(other)
     for col in range(2):
-
-        def fill_own(index, carry, col=col):
-            start = index * step
-            rows = pl.ds(pl.multiple_of(col * points + start, step), step)
-            local = pl.ds(pl.multiple_of(start, step), step)
-            block = block_of(rows, col, 0, col)
-            block = block + own_diagonal(start, points_col[rows, 2:3], points)
-            mats[col, local, 0:points] = block
-            cols = cols_of(0, col)
-            top[rows, cols], low[rows, cols] = split(block)
-            mats[col, local, points:ext] = covariance(
-                points_col[rows, 0:1], points_col[rows, 1:2],
-                ext_row[col, 0:1], ext_row[col, 1:2],
-            )
-            return carry
-
-        lax.fori_loop(0, points // step, fill_own, 0)
 
         def fill_ext(index, carry, col=col):
             start = index * step
@@ -761,30 +765,37 @@
             local = pl.ds(pl.multiple_of(points + start, step), step)
             mine_x = ext_col[col, rows, 0:1]
             mine_y = ext_col[col, rows, 1:2]
-            noise = ext_col[col, rows, 2:3]
             mats[col, local, 0:points] = covariance(
                 mine_x, mine_y, info[0, col, 0:1], info[0, col, 1:2]
             )
             block = covariance(mine_x, mine_y, ext_row[col, 0:1], ext_row[col, 1:2])
-            mats[col, local, points:ext] = block + own_diagonal(start, noise, borrowed)
+            mats[col, local, points:ext] = block + own_diagonal(
+                start, ext_col[col, rows, 2:3], borrowed
+            )
             return carry
 
         lax.fori_loop(0, borrowed // step, fill_ext, 0)
+        mats[col, 0:points, points:ext] = jnp.transpose(mats[col, points:ext, 0:points])
 
     def joined(first, second, both):
         return mm(
             jnp.concatenate([first, second], axis=1), jnp.concatenate([both, both], axis=0)
         )
 
+    close = 1 - lax.rem(my_x, 2)
+    distant = 1 - close
+
     def request(turn, value):
         both = wide(value)
-        wanted = folded(mm(pick[...], both))
-        own_asked[...] = wanted[: 2 * borrowed]
         moves = []
-        for index, side in enumerate(SIDES):
-            asked[turn, index] = wanted[2 * (index + 1) * borrowed : 2 * (index + 2) * borrowed]
-            moves.append(send(asked.at[turn, index], got.at[turn, 1 - index], side))
+        for side in (distant, close):
+            rows = pl.ds(pl.multiple_of(2 * (1 + side) * borrowed, borrowed), 2 * borrowed)
+            asked[turn, side] = folded(mm(pick[rows, :], both))
+            moves.append(send(asked.at[turn, side], got.at[turn, 1 - side], 2 * side - 1))
+        own_asked[...] = folded(mm(pick[: 2 * borrowed, :], both))
         return both, moves
+
+    piece = total // CUTS
 
     def solve(turn, both, moves, meanwhile=lambda: None):
         for col in range(2):
@@ -801,8 +812,7 @@
                 + joined(inv_top[col, points:, points:], inv_low[col, points:, points:], loaned[col])
             )
         returns = [
-            send(tails.at[turn], back.at[turn, 1 - index], side)
-            for index, side in enumerate(SIDES)
+            send(tails.at[turn], back.at[turn, 1 - side], 2 * side - 1) for side in (distant, close)
         ]
         owned = mm(put[:, : 2 * borrowed], wide(tails[turn]))
         for col in range(2):
@@ -816,36 +826,34 @@
         for move in returns:
             move.wait_recv()
         came = jnp.concatenate([wide(back[turn, 0]), wide(back[turn, 1])], axis=0)
-        basis[turn] = basis[turn] + folded(mm(put[:, 2 * borrowed :], came))
-
-    piece = total // CUTS
-    close = 1 - lax.rem(my_x, 2)
-
-    def apply(turn, meanwhile=lambda: None):
-        first = counter[0]
+        moves = []
         for cut in range(CUTS):
-            rows = pl.ds(cut * piece, piece)
-            for index, side in enumerate(SIDES):
-                send(basis.at[turn, rows], window.at[turn, 1 - index, rows], side)
+            rows = slice(cut * piece, (cut + 1) * piece)
+            basis[turn, rows] = basis[turn, rows] + folded(mm(put[rows, 2 * borrowed :], came))
+            for side in (distant, close):
+                here = pl.ds(cut * piece, piece)
+                moves.append(
+                    send(basis.at[turn, here], window.at[turn, 1 - side, here], 2 * side - 1)
+                )
+        return moves
+
+    def apply(turn, moves, meanwhile=lambda: None):
         send_far(turn, basis)
-
-        def landed(cut, index):
-            place = window.at[turn, index, pl.ds(cut * piece, piece)]
-            semaphore = recv_sem.at[first + 2 * cut + 1 - index]
-            pltpu.make_async_copy(place, place, semaphore).wait()
-
         accum[...] = joined(top[:, :total], low[:, :total], wide(basis[turn]))
         meanwhile()
-        for cut in range(CUTS):
-            landed(cut, close)
+        for move in moves[1::2]:
+            move.wait_recv()
         cols = pl.ds(pl.multiple_of((close + 1) * total, total), total)
         accum[...] = accum[...] + joined(top[:, cols], low[:, cols], wide(window[turn, close]))
         for cut in range(CUTS):
-            landed(cut, 1 - close)
-            both = wide(window[turn, 1 - close, cut * piece : (cut + 1) * piece])
-            cols = pl.ds(pl.multiple_of((2 - close) * total + cut * piece, piece), piece)
-            accum[...] = accum[...] + joined(top[:, cols], low[:, cols], both)
-        images[turn] = folded(accum[...])
+            moves[2 * cut].wait_recv()
+            both = wide(window[turn, distant, cut * piece : (cut + 1) * piece])
+            cols = pl.ds(pl.multiple_of((distant + 1) * total + cut * piece, piece), piece)
+            reached = accum[...] + joined(top[:, cols], low[:, cols], both)
+            if cut < CUTS - 1:
+                accum[...] = reached
+            else:
+                images[turn] = folded(reached)
 
     far_moves = []
 
@@ -892,15 +900,13 @@
     invert_both(mats, pivots, crossing)
     for col in range(2):
         inv_top[col], inv_low[col] = split(mats[col])
-    solve(0, *asking, fill_cross)
-    apply(0, fill_sides)
+    apply(0, solve(0, *asking, fill_cross), fill_sides)
     send_far(0, images)
     summing = begin_sum(
         0, [inner(start_res[...], basis[0]), inner(basis[0], images[0]), nothing]
     )
     asking = request(1, images[0])
-    solve(1, *asking)
-    apply(1)
+    apply(1, solve(1, *asking))
     send_far(1, images)
     gamma_0, curve_0, _ = end_sum(0, summing)
     alpha_0 = over(gamma_0, curve_0)
@@ -916,7 +922,7 @@
             inner(work[...], images[0]),
         ],
     )
-    solve(2, *asking)
+    moves = solve(2, *asking)
     gamma_1, curve_1, mixed_1 = end_sum(1, summing)
     beta_1 = over(gamma_1, gamma_0)
     curve_1 = curve_of(curve_1, mixed_1, beta_1, curve_0)
@@ -928,7 +934,7 @@
         last[...] = work[...] - step_1 * (basis[2] + ratio_1 * basis[1])
         work_image[...] = work_image[...] - (step_1 * ratio_1) * images[1]
 
-    apply(2, prepare)
+    apply(2, moves, prepare)
     send_far(2, images)
     last_image = work_image[...] - step_1 * images[2]
     summing = begin_sum(
@@ -1037,9 +1043,11 @@
     return pl.pallas_call(
         paired_kernel,
         out_shape=(out, out),
-        in_specs=[VMEM] * 4,
+        in_specs=[pl.BlockSpec(memory_space=pl.ANY)] + [VMEM] * 3,
         out_specs=(VMEM, VMEM),
         scratch_shapes=[
+            f32(points, width),
+            pltpu.SemaphoreType.DMA,
             f32(3, 2, 8, points),
             f32(total, borrowed),
             f32(2, 8, borrowed),
@@ -1099,7 +1107,7 @@
         P("gx", "gy", None),
     )
     return jax.shard_map(
-        paired_shards if mesh.shape["gy"] == 2 else shards,
+        paired_shards if mesh.shape["gy"] == 2 and mesh.shape["gx"] % 2 == 0 else shards,
         mesh=mesh,
         in_specs=placed,
         out_specs=(P("gx", "gy", None, None), P("gx", "gy", None, None)),

time: 124 us -> 116 us (0.935)
  Pallas kernels: 120 us -> 113 us
    pallas_call x1, Pallas kernels: 120 us -> 113 us  [paired_solve(): pl.pallas_call(paired_kernel, out_shape=(out, out), in_specs=[pl.BlockSpe...]
where the time goes in v2:
time: 116 us
  Pallas kernels  113 us (97%)
  local copies, waits for them, and re-layouts  2.72 us (2%)
    pallas_call x1, Pallas kernels, paired_solve(): pl.pallas_call(paired_kernel, out_shape=(out, out), in_specs=[pl.BlockSpe...  113 us
    unnamed x4, local copies, waits for them, and re-layouts  2.72 us

profile of v2, /device:TPU:0, one launch (start us, length us, event | category | flops | bytes accessed | tf_op | source)
XLA Modules:
  0.0 115.9 jit_solution(8083483566848007394)
XLA Ops:
  0.6 112.5 %shard_map.59 = (f32[512,256]{1,0:T(8,128)}, f32[512,256]{1,0:T(8,128)}) custom-call(f32[512,256]{1,0:T(8,128)} %bitcast.6, f32[2,512]{1,0:T(2,128)} %bitcast.9, f32[1,512]{1,0:T(1,128)} %bitcast.10, s32[1,128]{1,0:T(1,128)} %bitcast.11), custom_call_target="tpu_custom_call" | custom-call | tf_op jit(solution)/shard_map/pallas_call | solution.py:1043
  113.1 0.0 copy-start
  113.2 1.9 %copy.8 = f32[1,1,512,256]{3,2,1,0:T(8,128)} copy(f32[1,1,512,256]{3,2,1,0:T(8,128)} %bitcast.8) | data formatting | bytes 1048576
  115.1 0.0 copy-done
  115.1 0.8 copy.9
Async XLA Ops:
  113.1 1.9 %copy-start = (f32[512,256]{1,0:T(8,128)S(1)}, f32[512,256]{1,0:T(8,128)}, u32[]{:S(2)}) copy-start(f32[512,256]{1,0:T(8,128)} %get-tuple-element.5) | copy-start | bytes 1572868

commit v3 on v2

--- a/solution.py
+++ b/solution.py
@@ -690,17 +690,16 @@
     def hot(first, second):
         return jnp.where(first == second, 1.0, 0.0).astype(jnp.bfloat16)
 
-    for side in (0, -1, 1):
+    def mark(side, col):
         place = row_of_side[side]
-        for col in range(2):
-            facts_here = info[place, col]
-            row_ids = facts_here[3:4, :borrowed] - offset_of(1 - side, col)
-            slots_here = pl.ds((2 * place + col) * borrowed, borrowed)
-            put[:, slots_here] = hot(point_down, row_ids)
-            turned = jnp.transpose(
-                jnp.concatenate([facts_here[:, :borrowed], square_pad], axis=0)
-            )
-            pick[slots_here, :] = hot(turned[:, 3:4] - offset_of(1 - side, col), point_across)
+        facts_here = info[place, col]
+        row_ids = facts_here[3:4, :borrowed] - offset_of(1 - side, col)
+        slots_here = pl.ds((2 * place + col) * borrowed, borrowed)
+        put[:, slots_here] = hot(point_down, row_ids)
+        turned = jnp.transpose(jnp.concatenate([facts_here[:, :borrowed], square_pad], axis=0))
+        pick[slots_here, :] = hot(turned[:, 3:4] - offset_of(1 - side, col), point_across)
+
+    marks = [(side, col) for side in (0, -1, 1) for col in range(2)]
 
     def parts_of(place):
         row = jnp.concatenate([info[place, 0], info[place, 1]], axis=1)
@@ -754,7 +753,7 @@
         fill(lambda col: [(0, 1 - col)], 64)
 
     def fill_sides():
-        fill(lambda col: [(side, source) for side in SIDES for source in range(2)], 32)
+        fill(lambda col: [(side, source) for side in SIDES for source in range(2)], 64)
 
     fill_own(other)
     for col in range(2):
@@ -895,9 +894,13 @@
 
     nothing = jnp.zeros((1, lanes), jnp.float32)
 
-    rhs_move.wait_recv()
-    asking = request(0, start_res[...])
-    invert_both(mats, pivots, crossing)
+    def ask_first():
+        rhs_move.wait_recv()
+        return request(0, start_res[...])
+
+    asking = invert_both(
+        mats, pivots, crossing, lambda: marks and mark(*marks.pop(0)), ask_first
+    )
     for col in range(2):
         inv_top[col], inv_low[col] = split(mats[col])
     apply(0, solve(0, *asking, fill_cross), fill_sides)
@@ -980,7 +983,7 @@
         move.wait_send()
 
 
-def invert_both(mats, pivots, crossing):
+def invert_both(mats, pivots, crossing, beside, meanwhile):
     size, step = mats.shape[1], pivots.shape[1]
     rows = lax.broadcasted_iota(jnp.int32, (size, step), 0)
     lanes = lax.broadcasted_iota(jnp.int32, (size, step), 1)
@@ -1025,10 +1028,15 @@
         return carry
 
     first = slice(0, step)
-    for which, pivot in enumerate(pivot_inverses([mats[at, first, first] for at in range(2)])):
-        pivots[which] = pivot
-    lax.fori_loop(0, size // step - 1, looped, 0)
-    eliminate(size // step - 1, False)
+    found = pivot_inverses([mats[which, first, first] for which in range(2)], beside)
+    for which in range(2):
+        pivots[which] = found[which]
+    last = size // step - 1
+    lax.fori_loop(0, last // 2, looped, 0)
+    result = meanwhile()
+    lax.fori_loop(last // 2, last, looped, 0)
+    eliminate(last, False)
+    return result
 
 
 def paired_solve(right_side, coords, noise, intersect):
@@ -1043,7 +1051,7 @@
     return pl.pallas_call(
         paired_kernel,
         out_shape=(out, out),
-        in_specs=[pl.BlockSpec(memory_space=pl.ANY)] + [VMEM] * 3,
+        in_specs=[pl.BlockSpec(memory_space=pltpu.HBM)] + [VMEM] * 3,
         out_specs=(VMEM, VMEM),
         scratch_shapes=[
             f32(points, width),
@@ -1083,7 +1091,7 @@
             pltpu.SemaphoreType.DMA((moves,)),
         ],
         compiler_params=pltpu.CompilerParams(
-            collective_id=0, has_side_effects=True, vmem_limit_bytes=58 * 1024 * 1024
+            collective_id=0, has_side_effects=True, vmem_limit_bytes=52 * 1024 * 1024
         ),
     )(right_side, coords, noise, intersect)
 

time: 116 us -> 113 us (0.974)
  Pallas kernels: 113 us -> 109 us
    pallas_call x1, Pallas kernels: 113 us -> 109 us  [paired_solve(): pl.pallas_call(paired_kernel, out_shape=(out, out), in_specs=[pl.BlockSpe...]
    unnamed x4 -> x10, local copies, waits for them, and re-layouts: 2.72 us -> 3.31 us
where the time goes in v3:
time: 113 us
  Pallas kernels  109 us (96%)
  local copies, waits for them, and re-layouts  3.31 us (3%)
    pallas_call x1, Pallas kernels, paired_solve(): pl.pallas_call(paired_kernel, out_shape=(out, out), in_specs=[pl.BlockSpe...  109 us
    unnamed x10, local copies, waits for them, and re-layouts  3.31 us

profile of v3, /device:TPU:0, one launch (start us, length us, event | category | flops | bytes accessed | tf_op | source)
XLA Modules:
  0.0 113.2 jit_solution(12235688037185407497)
XLA Ops:
  0.6 0.0 copy-start.1
  0.6 0.0 copy-start.2
  0.7 0.0 copy-start.3
  0.7 0.7 copy-done.1
  1.3 0.0 copy-done.2
  1.3 0.0 copy-done.3
  1.3 0.0 copy-start
  1.3 1.0 copy-done
  2.4 109.2 %shard_map.59 = (f32[512,256]{1,0:T(8,128)S(1)}, f32[512,256]{1,0:T(8,128)S(1)}) custom-call(f32[512,256]{1,0:T(8,128)S(1)} %bitcast.6, f32[2,512]{1,0:T(2,128)S(1)} %bitcast.9, f32[1,512]{1,0:T(1,128)S(1)} %bitcast.10, s32[1,128]{1,0:T(1,128)S(1)} %bitcast.11), custom_call_target="tpu_custom_call" | custom-call | tf_op jit(solution)/shard_map/pallas_call | solution.py:1051
  111.6 0.8 copy.8
  112.4 0.8 copy.9
Async XLA Ops:
  0.6 0.7 copy-start.1
  0.6 0.7 copy-start.2
  0.7 0.7 copy-start.3
  1.3 1.0 copy-start
